TPU v7x, 32 devices: a whole 2x2x4 slice. The times are simulated.
32 devices in a mesh: seq: 8 (over z, y), grp: 4 (over x, core).
Axes of the slice: x: 2, y: 2, z: 4, core: 2. Of those that a mesh axis runs over, the one named last changes fastest.
Arguments:
- query_nope: bfloat16 [4, 2, 128, 128], P(None, None, 'seq'), may hold values from -12.859821 to 12.859821
- query_rope: bfloat16 [4, 2, 128, 64], P(None, None, 'seq'), may hold values from -150 to 150
- latent_cache: bfloat16 [4, 8192, 576], P(None, ('seq', 'grp')), may hold values from -5 to 5
- lengths: int32 [4], replicated, may hold values from 4096 to 8192
- key_weight: bfloat16 [128, 128, 512], P('seq'), may hold values from -0.5 to 0.5
- value_weight: bfloat16 [128, 512, 128], P('seq'), may hold values from -0.25 to 0.25
- output_weight: bfloat16 [16384, 7168], P('seq', 'grp'), may hold values from -0.0625 to 0.0625
Outputs:
- mixed: bfloat16 [4, 2, 7168], P(None, None, ('grp', 'seq'))
All inputs are finite; a program needn't handle non-finite values.
Results may differ from a plain program's by a relative error of at most 0.0095.
Values may be sent and summed in bfloat16 or wider, within the bound.
No kernel may reach another device: no remote copies, remote signals or barrier semaphores. Data moves between devices by JAX's collectives and lax.ppermute only.
A program may use at most 64 MiB of HBM per device.

v0:
```python
import jax
import jax.numpy as jnp
from jax import lax
from jax.sharding import PartitionSpec as P

NEGATIVE = -1e30


def joined(part, axis, combine):
    gathered = jax.tree.map(lambda a: lax.all_gather(a, axis), part)

    def take(source):
        return jax.tree.map(lambda a: lax.dynamic_index_in_dim(a, source, 0, False), gathered)

    return lax.fori_loop(
        1, lax.axis_size(axis), lambda source, state: combine(state, take(source)), take(0)
    )


def shard_partial(queries, cache_block, limits, offset, factor, latent_width):
    raw_score = (
        jnp.einsum("bqhd,bpd->bqhp", queries, cache_block, preferred_element_type=jnp.float32)
        * factor
    )
    places = offset + lax.broadcasted_iota(jnp.int32, (1, 1, cache_block.shape[1]), 2)
    visible = places < limits[:, :, None]
    scores = jnp.where(visible[:, :, None, :], raw_score, NEGATIVE)
    maxima = jnp.max(scores, axis=-1)
    powers = jnp.exp(scores - maxima[..., None])
    totals = jnp.sum(powers, axis=-1)
    weights = powers.astype(jnp.bfloat16)
    summed = jnp.einsum(
        "bqhp,bpd->bqhd",
        weights,
        cache_block[:, :, :latent_width],
        preferred_element_type=jnp.float32,
    )
    return (maxima, totals, (summed / totals[..., None]).astype(jnp.bfloat16))


def merge_sources(partials, maxima, totals):
    highest = jnp.max(maxima, axis=0)
    shares = totals * jnp.exp(maxima - highest[None])
    summed = jnp.sum(shares, axis=0)
    numerator = jnp.sum(shares[..., None] * partials.astype(jnp.float32), axis=0)
    return (highest, summed, numerator / summed[..., None])


def merge_tuple(received):
    return merge_sources(received[0], received[1], received[2])


def join_pairs(earlier, later):
    highest = jnp.maximum(earlier[0], later[0])
    left_share = earlier[1] * jnp.exp(earlier[0] - highest)
    right_share = later[1] * jnp.exp(later[0] - highest)
    summed = left_share + right_share
    blended = (left_share[..., None] * earlier[2] + right_share[..., None] * later[2]) / summed[
        ..., None
    ]
    return (highest, summed, blended)


def absorb(query_nope, query_rope, key_weight):
    absorbed = jnp.einsum(
        "bqhn,hnd->bqhd", query_nope, key_weight, preferred_element_type=jnp.float32
    )
    return jnp.concatenate([absorbed.astype(jnp.bfloat16), query_rope], axis=-1)


def up_project(latent_out, value_weight):
    values = jnp.einsum(
        "bqhd,hde->bqhe", latent_out, value_weight, preferred_element_type=jnp.float32
    ).astype(jnp.bfloat16)
    return values.reshape(values.shape[0], values.shape[1], values.shape[2] * values.shape[3])


def shards(query_nope, query_rope, latent_cache, lengths, key_weight, value_weight, output_weight):
    latent_width = key_weight.shape[2]
    factor = float(query_nope.shape[3] + query_rope.shape[3]) ** (-0.5)
    positions = latent_cache.shape[1]
    drafts = query_nope.shape[1]
    offset = (lax.axis_index("seq") * lax.axis_size("grp") + lax.axis_index("grp")) * positions
    limits = lengths[:, None] - drafts + 1 + lax.broadcasted_iota(jnp.int32, (1, drafts), 1)
    own_queries = absorb(query_nope, query_rope, key_weight)
    maxima, totals, partials = shard_partial(
        lax.all_gather(own_queries, "seq", axis=2, tiled=True),
        latent_cache,
        limits,
        offset,
        factor,
        latent_width,
    )
    partials, maxima, totals = (partials, maxima, totals)
    sources = (partials[None], maxima[None], totals[None])
    gathered = merge_tuple(
        (
            lax.all_to_all(
                sources[0].astype(jnp.float32), "seq", split_axis=3, concat_axis=0, tiled=True
            ).astype(jnp.bfloat16),
            lax.all_to_all(sources[1], "seq", split_axis=3, concat_axis=0, tiled=True),
            lax.all_to_all(sources[2], "seq", split_axis=3, concat_axis=0, tiled=True),
        )
    )
    highest, summed, blended = joined((gathered[0], gathered[1], gathered[2]), "grp", join_pairs)
    values = up_project(blended.astype(jnp.bfloat16), value_weight)
    head_terms = jnp.dot(values, output_weight, preferred_element_type=jnp.float32)
    reduced = lax.psum_scatter(head_terms, "seq", scatter_dimension=2, tiled=True)
    return reduced.astype(jnp.bfloat16)


def solution(mesh):
    in_specs = (
        P(None, None, "seq", None),
        P(None, None, "seq", None),
        P(None, ("seq", "grp"), None),
        P(),
        P("seq", None, None),
        P("seq", None, None),
        P("seq", "grp"),
    )
    out_specs = P(None, None, ("grp", "seq"))
    return jax.shard_map(shards, mesh=mesh, in_specs=in_specs, out_specs=out_specs, check_vma=False)
```

profile of v0, /device:TPU:0, one launch (start us, length us, event | category | flops | bytes accessed | tf_op | source)
XLA Modules:
  0.0 212.3 jit_solution(17703678175560071938)
XLA Ops:
  6.5 0.9 copy.29
  7.5 0.7 copy-done
  8.1 1.1 fusion.18
  9.3 0.8 pad_maximum_fusion
  10.2 44.5 %all-gather.5.cloned.1.call-done = bf16[4,2,128,576]{3,0,1,2:T(4,128)(2,1)} async-done(((bf16[4,2,16,576]{3,0,1,2:T(4,128)(2,1)}), bf16[4,2,128,576]{3,0,1,2:T(4,128)(2,1)}) %all-gather.5.cloned.1.call-update) | async-done | bytes 1179664 | tf_op jit(solution)/shard_map/all_gather | solution.py:87
  54.7 2.4 %fusion.42 = (f32[4,2,128]{2,1,0:T(2,128)S(1)}, f32[4,2,128,256]{3,2,1,0:T(8,128)S(1)}) fusion(bf16[4,256,576]{1,2,0:T(8,128)(2,1)} %param.11, bf16[4,2,128,576]{3,0,1,2:T(4,128)(2,1)} %all-gather.5.cloned.1.call-done, pred[4,2,256]{2,1,0:T(4,128)(4,1)S(1)} %broadcast_compare_fusion), kind=kOutput, calls=%fused_computation.50 | convolution fusion | flops 302775296 | bytes 3414016 | tf_op jit(solution)/shard_map/bqhd,bpd->bqhp/dot_general | solution.py:22
  57.1 0.4 fusion.30
  57.5 0.2 copy.34
  57.7 0.8 reshape.85
  58.5 3.4 %all-to-all-start.1 = ((f32[8,1,128]{2,1,0:T(1,128)}), f32[8,1,128]{2,1,0:T(1,128)S(1)}, u32[]{:S(2)}, u32[]{:S(2)}) async-start(f32[8,1,128]{2,1,0:T(1,128)} %reshape.85), calls=%async_computation.1 | async-start | bytes 8192 | tf_op jit(solution)/shard_map/all_to_all | solution.py:102
  61.9 0.2 copy.31
  62.1 0.8 reshape.83
  62.9 5.5 %all-to-all-done.1 = f32[8,1,128]{2,1,0:T(1,128)S(1)} async-done(((f32[8,1,128]{2,1,0:T(1,128)}), f32[8,1,128]{2,1,0:T(1,128)S(1)}, u32[]{:S(2)}, u32[]{:S(2)}) %all-to-all-start.1) | async-done | bytes 4128 | tf_op jit(solution)/shard_map/all_to_all | solution.py:102
  68.4 3.3 %all-to-all-start = ((f32[8,1,128]{2,1,0:T(1,128)}), f32[8,1,128]{2,1,0:T(1,128)S(1)}, u32[]{:S(2)}, u32[]{:S(2)}) async-start(f32[8,1,128]{2,1,0:T(1,128)} %reshape.83), calls=%async_computation | async-start | bytes 8192 | tf_op jit(solution)/shard_map/all_to_all | solution.py:101
  71.7 1.7 fusion.11
  73.5 2.1 copy.38
  75.6 2.5 %all-to-all-done = f32[8,1,128]{2,1,0:T(1,128)S(1)} async-done(((f32[8,1,128]{2,1,0:T(1,128)}), f32[8,1,128]{2,1,0:T(1,128)S(1)}, u32[]{:S(2)}, u32[]{:S(2)}) %all-to-all-start) | async-done | bytes 4128 | tf_op jit(solution)/shard_map/all_to_all | solution.py:101
  78.1 3.6 %all-to-all-start.2 = ((bf16[1,4,2,128,512]{4,2,1,0,3:T(2,128)(2,1)}), bf16[1,4,2,128,512]{4,2,1,0,3:T(2,128)(2,1)S(1)}, u32[]{:S(2)}, u32[]{:S(2)}) async-start(bf16[1,4,2,128,512]{4,2,1,0,3:T(2,128)(2,1)} %copy.38), calls=%async_computation.2 | async-start | bytes 2097152 | tf_op jit(solution)/shard_map/all_to_all | solution.py:98
  81.7 0.5 broadcast.51
  82.2 0.7 reduce.2
  82.9 0.2 reshape.86
  83.1 1.6 copy.35
  84.7 0.7 reduce.1
  85.4 0.2 reshape.84
  85.6 0.9 copy.32
  86.6 1.8 fusion.40
  88.4 16.5 %all-to-all-done.2 = bf16[1,4,2,128,512]{4,2,1,0,3:T(2,128)(2,1)S(1)} async-done(((bf16[1,4,2,128,512]{4,2,1,0,3:T(2,128)(2,1)}), bf16[1,4,2,128,512]{4,2,1,0,3:T(2,128)(2,1)S(1)}, u32[]{:S(2)}, u32[]{:S(2)}) %all-to-all-start.2) | async-done | bytes 1048608 | tf_op jit(solution)/shard_map/all_to_all | solution.py:98
  104.9 2.3 %fusion.7 = f32[4,2,16,512]{3,1,0,2:T(2,128)S(1)} fusion(bf16[1,4,2,8,16,512]{5,2,1,4,3,0:T(2,128)(2,1)S(1)} %bitcast.108, f32[8,4,2,16]{2,1,3,0:T(4,128)} %get-tuple-element.201), kind=kLoop, calls=%fused_computation.13 | loop fusion | flops 1507328 | bytes 1314816 | tf_op jit(solution)/shard_map/reduce_sum | solution.py:45
  107.2 0.2 bitcast_divide_fusion
  107.3 0.9 copy.39
  108.3 0.1 copy.33
  108.4 0.1 copy.36
  108.5 5.2 %all-gather.1 = f32[16,2,16]{2,1,0:T(2,128)S(1)} all-gather(f32[4,2,16]{2,1,0:T(2,128)S(1)} %copy.36), channel_id=3, replica_groups=mesh['seq'=8,'grp'=4] {'grp'}, dimensions={0}, use_global_device_ids=true | all-gather | bytes 2560 | tf_op jit(solution)/shard_map/all_gather | solution.py:10
  113.7 5.2 %all-gather = f32[16,2,16]{2,1,0:T(2,128)S(1)} all-gather(f32[4,2,16]{2,1,0:T(2,128)S(1)} %copy.33), channel_id=2, replica_groups=mesh['seq'=8,'grp'=4] {'grp'}, dimensions={0}, use_global_device_ids=true | all-gather | bytes 2560 | tf_op jit(solution)/shard_map/all_gather | solution.py:10
  118.9 5.1 %all-gather.7.cloned.1.call-done = f32[4,4,2,16,512]{4,3,2,1,0:T(8,128)} async-done(((f32[1,4,2,16,512]{4,3,2,1,0:T(8,128)}), f32[4,4,2,16,512]{4,3,2,1,0:T(8,128)}) %all-gather.7.cloned.1.call-update) | async-done | bytes 1048592 | tf_op jit(solution)/shard_map/all_gather | solution.py:10
  124.0 1.0 slice_bitcast_fusion
  124.9 3.5 %while.19 = (s32[]{:T(128)}, f32[4,2,16]{2,1,0:T(2,128)S(1)}, f32[4,2,16]{2,1,0:T(2,128)S(1)}, f32[4,2,16,512]{3,2,1,0:T(8,128)S(1)}, f32[4,4,2,16]{3,2,1,0:T(2,...) while((s32[]{:T(128)}, f32[4,2,16]{2,1,0:T(2,128)S(1)}, ...), condition=%wide.region_6.7_spmd, body=%wide.region_5.6_spmd.sunk | while | flops 262917 | bytes 792207 | solution.py:15
  125.0 1.1 fusion.46
  126.2 1.1 fusion.46
  127.3 1.1 fusion.46
  128.4 2.0 fusion.24
  130.5 4.2 %fusion.3 = f32[4,2,1792]{2,0,1:T(4,128)S(1)} fusion(bf16[2048,1792]{1,0:T(8,128)(2,1)} %param.15, bf16[16,2,1,4,128]{4,3,2,1,0:T(4,128)(2,1)S(1)} %fusion.24), kind=kOutput, calls=%fused_computation.8 | convolution fusion | flops 58720256 | bytes 7430144 | tf_op jit(solution)/shard_map/dot_general | solution.py:107
  134.7 2.3 %copy.49 = f32[4,2,1792]{0,1,2:T(2,128)} copy(f32[4,2,1792]{2,0,1:T(4,128)S(1)} %fusion.3) | data formatting | bytes 114688
  137.0 3.1 %reshape.81 = f32[1792,8]{1,0:T(8,128)} reshape(f32[1792,2,4]{2,1,0:T(2,128)} %bitcast.107) | data formatting | bytes 114688
  140.1 63.9 %reduce-scatter.4.cloned.1.call-done = f32[224,8]{1,0:T(8,128)} async-done(((f32[1792,8]{1,0:T(8,128)}), f32[224,8]{1,0:T(8,128)}) %reduce-scatter.4.cloned.1.call-update) | async-done | bytes 7184
  204.0 1.0 reshape.82
  205.0 0.1 copy.50
  205.1 0.6 copy.43
  (20 shorter events, 0.5 us)
Async XLA Ops:
  6.5 1.6 copy-start
  6.5 3.5 %copy-start.1 = (s32[4]{0:T(128)S(1)}, s32[4]{0:T(128)}, u32[]{:S(2)}) copy-start(s32[4]{0:T(128)} %param.12) | copy-start | bytes 52
  6.5 48.2 %all-gather.5.cloned.1.call-start = ((), (), s32[]{:S(2)}) async-start(), calls=%async_computation.4 | async-start | bytes 1474560 | tf_op jit(solution)/shard_map/all_gather | solution.py:87
  58.5 9.9 %all-to-all-start.1 = ((f32[8,1,128]{2,1,0:T(1,128)}), f32[8,1,128]{2,1,0:T(1,128)S(1)}, u32[]{:S(2)}, u32[]{:S(2)}) async-start(f32[8,1,128]{2,1,0:T(1,128)} %reshape.85), calls=%async_computation.1 | async-start | bytes 8192 | tf_op jit(solution)/shard_map/all_to_all | solution.py:102
  68.4 9.7 %all-to-all-start = ((f32[8,1,128]{2,1,0:T(1,128)}), f32[8,1,128]{2,1,0:T(1,128)S(1)}, u32[]{:S(2)}, u32[]{:S(2)}) async-start(f32[8,1,128]{2,1,0:T(1,128)} %reshape.83), calls=%async_computation | async-start | bytes 8192 | tf_op jit(solution)/shard_map/all_to_all | solution.py:101
  78.1 26.8 %all-to-all-start.2 = ((bf16[1,4,2,128,512]{4,2,1,0,3:T(2,128)(2,1)}), bf16[1,4,2,128,512]{4,2,1,0,3:T(2,128)(2,1)S(1)}, u32[]{:S(2)}, u32[]{:S(2)}) async-start(bf16[1,4,2,128,512]{4,2,1,0,3:T(2,128)(2,1)} %copy.38), calls=%async_computation.2 | async-start | bytes 2097152 | tf_op jit(solution)/shard_map/all_to_all | solution.py:98
  81.6 42.3 %all-gather.7.cloned.1.call-start = ((), (), s32[]{:S(2)}) async-start(), calls=%async_computation.5 | async-start | bytes 1310720 | tf_op jit(solution)/shard_map/all_gather | solution.py:10
  108.2 95.8 %reduce-scatter.4.cloned.1.call-start = ((), (), s32[]{:S(2)}) async-start(), calls=%async_computation.6 | async-start | bytes 1032192
Sparse Core Ops, SparseCore 0:
  10.2 44.5 all-gather.4
  108.4 15.5 all-gather.6
  140.3 63.6 reduce-scatter.3
where the time goes:
time: 213 us; the launch traced here: 212 us
  waiting for transfers between devices  138 us (65%)
  local copies, waits for them, and re-layouts  18.2 us (9%)
  between operations  13.3 us (6%)
  matrix products  11.5 us (5%)
  starting transfers between devices  10.4 us (5%)
  blocking collectives  10.4 us (5%)
  other arithmetic  10.3 us (5%)
    unnamed x4, waiting for transfers between devices  63.9 us
    all_gather x1, waiting for transfers between devices, shards(): lax.all_gather(own_queries, 'seq', axis=2, tiled=True)  44.5 us
    all_to_all x1, waiting for transfers between devices, shards(): lax.all_to_all(sources[0].astype(jnp.float32), 'seq', split_axis=3, conca...  16.5 us
    all_gather x2, blocking collectives, joined(): gathered = jax.tree.map(lambda a: lax.all_gather(a, axis), part)  10.4 us
    unnamed x13, local copies, waits for them, and re-layouts  10.2 us
    all_to_all x1, waiting for transfers between devices, shards(): lax.all_to_all(sources[2], 'seq', split_axis=3, concat_axis=0, tiled=True)  5.53 us
    all_gather x1, waiting for transfers between devices, joined(): gathered = jax.tree.map(lambda a: lax.all_gather(a, axis), part)  5.1 us
  transfers between devices with their start and end apart: 6, of which 6 were waited for; matrix products, arithmetic and copies ran while one was open for 6% of the time, Pallas kernels for 0%

commit v1 on v0

--- a/solution.py
+++ b/solution.py
@@ -95,8 +95,16 @@
     sources = (partials[None], maxima[None], totals[None])
     gathered = merge_tuple(
         (
-            lax.all_to_all(
-                sources[0].astype(jnp.float32), "seq", split_axis=3, concat_axis=0, tiled=True
+            jnp.concatenate(
+                lax.all_to_all(
+                    jnp.stack(
+                        jnp.split(sources[0].astype(jnp.float32), lax.axis_size("seq"), axis=3)
+                    ),
+                    "seq",
+                    0,
+                    0,
+                ),
+                axis=0,
             ).astype(jnp.bfloat16),
             lax.all_to_all(sources[1], "seq", split_axis=3, concat_axis=0, tiled=True),
             lax.all_to_all(sources[2], "seq", split_axis=3, concat_axis=0, tiled=True),

time: 213 us -> 212 us (level)
  waiting for transfers between devices: 138 us -> 143 us
  other arithmetic: 10.3 us -> 7.18 us
    all_to_all x1, waiting for transfers between devices: 16.5 us -> 19.8 us  [shards(): lax.all_to_all(jnp.stack(jnp.split(sources[0].astype(jnp.float32), lax.ax...]
    unnamed x13 -> x26, local copies, waits for them, and re-layouts: 10.2 us -> 13 us
  transfers between devices with their start and end apart: 6 -> 6, of which waited for: 6 -> 6; matrix products, arithmetic and copies ran while one was open for 6% -> 3% of each run, Pallas kernels for 0% -> 0%
where the time goes in v1:
time: 212 us; the launch traced here: 211 us
  waiting for transfers between devices  143 us (67%)
  local copies, waits for them, and re-layouts  16.7 us (8%)
  between operations  13.3 us (6%)
  starting transfers between devices  10.4 us (5%)
  matrix products  10.4 us (5%)
  blocking collectives  10.4 us (5%)
  other arithmetic  7.18 us (3%)
    unnamed x4, waiting for transfers between devices  63.9 us
    all_gather x1, waiting for transfers between devices, shards(): lax.all_gather(own_queries, 'seq', axis=2, tiled=True)  44.5 us
    all_to_all x1, waiting for transfers between devices, shards(): lax.all_to_all(jnp.stack(jnp.split(sources[0].astype(jnp.float32), lax.ax...  19.8 us
    unnamed x26, local copies, waits for them, and re-layouts  13 us
    all_gather x2, blocking collectives, joined(): gathered = jax.tree.map(lambda a: lax.all_gather(a, axis), part)  10.4 us
    all_gather x1, waiting for transfers between devices, joined(): gathered = jax.tree.map(lambda a: lax.all_gather(a, axis), part)  5.3 us
    all_to_all x1, waiting for transfers between devices, shards(): lax.all_to_all(sources[2], 'seq', split_axis=3, concat_axis=0, tiled=True)  4.61 us
    all_to_all x1, waiting for transfers between devices, shards(): lax.all_to_all(sources[1], 'seq', split_axis=3, concat_axis=0, tiled=True)  4.44 us
  transfers between devices with their start and end apart: 6, of which 6 were waited for; matrix products, arithmetic and copies ran while one was open for 3% of the time, Pallas kernels for 0%

profile of v1, /device:TPU:0, one launch (start us, length us, event | category | flops | bytes accessed | tf_op | source)
XLA Modules:
  0.0 211.0 jit_solution(3330645228296328237)
XLA Ops:
  6.5 0.9 copy.32
  7.5 0.7 copy-done
  8.1 1.1 fusion.18
  9.3 0.8 pad_maximum_fusion
  10.2 0.1 broadcast_compare_fusion
  10.3 44.5 %all-gather.5.cloned.1.call-done = bf16[4,2,128,576]{3,0,1,2:T(4,128)(2,1)} async-done(((bf16[4,2,16,576]{3,0,1,2:T(4,128)(2,1)}), bf16[4,2,128,576]{3,0,1,2:T(4,128)(2,1)}) %all-gather.5.cloned.1.call-update) | async-done | bytes 1179664 | tf_op jit(solution)/shard_map/all_gather | solution.py:87
  54.8 2.5 %fusion.50 = (f32[4,2,128]{2,1,0:T(2,128)S(1)}, f32[4,2,128,256]{3,2,1,0:T(8,128)S(1)}) fusion(bf16[4,256,576]{1,2,0:T(8,128)(2,1)} %param.11, bf16[4,2,128,576]{3,0,1,2:T(4,128)(2,1)} %all-gather.5.cloned.1.call-done, pred[4,2,256]{2,1,0:T(4,128)(4,1)S(1)} %broadcast_compare_fusion), kind=kOutput, calls=%fused_computation.66 | convolution fusion | flops 302775296 | bytes 3414016 | tf_op jit(solution)/shard_map/bqhd,bpd->bqhp/dot_general | solution.py:22
  57.2 0.4 fusion.30
  57.6 0.5 fusion.11
  58.3 0.9 copy-done.2
  59.2 0.2 copy.36
  59.3 0.8 reshape.82
  60.1 3.4 %all-to-all-start.1 = ((f32[8,1,128]{2,1,0:T(1,128)}), f32[8,1,128]{2,1,0:T(1,128)S(1)}, u32[]{:S(2)}, u32[]{:S(2)}) async-start(f32[8,1,128]{2,1,0:T(1,128)} %reshape.82), calls=%async_computation.1 | async-start | bytes 8192 | tf_op jit(solution)/shard_map/all_to_all | solution.py:110
  63.5 0.9 fusion.34
  64.5 0.2 copy.34
  64.6 0.8 reshape.80
  65.4 4.6 %all-to-all-done.1 = f32[8,1,128]{2,1,0:T(1,128)S(1)} async-done(((f32[8,1,128]{2,1,0:T(1,128)}), f32[8,1,128]{2,1,0:T(1,128)S(1)}, u32[]{:S(2)}, u32[]{:S(2)}) %all-to-all-start.1) | async-done | bytes 4128 | tf_op jit(solution)/shard_map/all_to_all | solution.py:110
  70.0 3.3 %all-to-all-start = ((f32[8,1,128]{2,1,0:T(1,128)}), f32[8,1,128]{2,1,0:T(1,128)S(1)}, u32[]{:S(2)}, u32[]{:S(2)}) async-start(f32[8,1,128]{2,1,0:T(1,128)} %reshape.80), calls=%async_computation | async-start | bytes 8192 | tf_op jit(solution)/shard_map/all_to_all | solution.py:109
  73.3 0.9 fusion.33
  74.3 1.0 copy-done.1
  75.3 4.4 %all-to-all-done = f32[8,1,128]{2,1,0:T(1,128)S(1)} async-done(((f32[8,1,128]{2,1,0:T(1,128)}), f32[8,1,128]{2,1,0:T(1,128)S(1)}, u32[]{:S(2)}, u32[]{:S(2)}) %all-to-all-start) | async-done | bytes 4128 | tf_op jit(solution)/shard_map/all_to_all | solution.py:109
  79.7 3.6 %all-to-all-start.2 = ((bf16[8,1,4,2,16,512]{5,4,3,2,1,0:T(8,128)(2,1)}), bf16[8,1,4,2,16,512]{5,4,3,2,1,0:T(8,128)(2,1)S(1)}, u32[]{:S(2)}, u32[]{:S(2)}) async-start(bf16[8,1,4,2,16,512]{5,4,3,2,1,0:T(8,128)(2,1)} %copy-done.1), calls=%async_computation.2 | async-start | bytes 2097152 | tf_op jit(solution)/shard_map/all_to_all | solution.py:99
  83.3 0.5 broadcast.51
  83.8 0.7 reduce.2
  84.5 0.2 reshape.83
  84.7 0.2 copy.49
  84.9 0.7 reduce.1
  85.6 0.2 reshape.81
  85.8 0.2 copy.48
  86.1 19.8 %all-to-all-done.2 = bf16[8,1,4,2,16,512]{5,4,3,2,1,0:T(8,128)(2,1)S(1)} async-done(((bf16[8,1,4,2,16,512]{5,4,3,2,1,0:T(8,128)(2,1)}), bf16[8,1,4,2,16,512]{5,4,3,2,1,0:T(8,128)(2,1)S(1)}, u32[]{:S(2)}, u32[]{:S(2)}) %all-to-all-start.2) | async-done | bytes 1048608 | tf_op jit(solution)/shard_map/all_to_all | solution.py:99
  105.9 0.3 fusion.7
  106.2 0.8 bitcast_divide_fusion
  107.0 5.2 %all-gather.1 = f32[16,2,16]{2,1,0:T(2,128)S(1)} all-gather(f32[4,2,16]{2,1,0:T(2,128)S(1)} %get-tuple-element.200), channel_id=3, replica_groups=mesh['seq'=8,'grp'=4] {'grp'}, dimensions={0}, use_global_device_ids=true | all-gather | bytes 2560 | tf_op jit(solution)/shard_map/all_gather | solution.py:10
  112.2 5.2 %all-gather = f32[16,2,16]{2,1,0:T(2,128)S(1)} all-gather(f32[4,2,16]{2,1,0:T(2,128)S(1)} %bitcast_reduce_fusion), channel_id=2, replica_groups=mesh['seq'=8,'grp'=4] {'grp'}, dimensions={0}, use_global_device_ids=true | all-gather | bytes 2560 | tf_op jit(solution)/shard_map/all_gather | solution.py:10
  117.4 5.3 %all-gather.7.cloned.1.call-done = f32[4,4,2,16,512]{4,3,2,1,0:T(8,128)} async-done(((f32[1,4,2,16,512]{4,3,2,1,0:T(8,128)}), f32[4,4,2,16,512]{4,3,2,1,0:T(8,128)}) %all-gather.7.cloned.1.call-update) | async-done | bytes 1048592 | tf_op jit(solution)/shard_map/all_gather | solution.py:10
  122.7 1.0 slice_bitcast_fusion
  123.7 3.5 %while.19 = (s32[]{:T(128)}, f32[4,2,16]{2,1,0:T(2,128)S(1)}, f32[4,2,16]{2,1,0:T(2,128)S(1)}, f32[4,2,16,512]{3,2,1,0:T(8,128)S(1)}, f32[4,4,2,16]{3,2,1,0:T(2,...) while((s32[]{:T(128)}, f32[4,2,16]{2,1,0:T(2,128)S(1)}, ...), condition=%wide.region_6.7_spmd, body=%wide.region_5.6_spmd.sunk | while | flops 262917 | bytes 792215 | solution.py:15
  123.8 1.1 fusion.54
  124.9 1.1 fusion.54
  126.1 1.1 fusion.54
  127.2 2.0 fusion.24
  129.2 4.2 %fusion.3 = f32[4,2,1792]{2,0,1:T(4,128)S(1)} fusion(bf16[2048,1792]{1,0:T(8,128)(2,1)} %param.15, bf16[16,2,1,4,128]{4,3,2,1,0:T(4,128)(2,1)S(1)} %fusion.24), kind=kOutput, calls=%fused_computation.8 | convolution fusion | flops 58720256 | bytes 7430144 | tf_op jit(solution)/shard_map/dot_general | solution.py:115
  133.5 2.3 %copy.51 = f32[4,2,1792]{0,1,2:T(2,128)} copy(f32[4,2,1792]{2,0,1:T(4,128)S(1)} %fusion.3) | data formatting | bytes 114688
  135.7 3.1 %reshape.78 = f32[1792,8]{1,0:T(8,128)} reshape(f32[1792,2,4]{2,1,0:T(2,128)} %bitcast.134) | data formatting | bytes 114688
  138.9 63.8 %reduce-scatter.4.cloned.1.call-done = f32[224,8]{1,0:T(8,128)} async-done(((f32[1792,8]{1,0:T(8,128)}), f32[224,8]{1,0:T(8,128)}) %reduce-scatter.4.cloned.1.call-update) | async-done | bytes 7184
  202.7 1.0 reshape.79
  203.7 0.1 copy.52
  203.8 0.6 copy.43
  (31 shorter events, 0.5 us)
Async XLA Ops:
  6.5 1.6 copy-start
  6.5 3.6 %copy-start.4 = (s32[4]{0:T(128)S(1)}, s32[4]{0:T(128)}, u32[]{:S(2)}) copy-start(s32[4]{0:T(128)} %param.12) | copy-start | bytes 52
  6.5 48.2 %all-gather.5.cloned.1.call-start = ((), (), s32[]{:S(2)}) async-start(), calls=%async_computation.4 | async-start | bytes 1474560 | tf_op jit(solution)/shard_map/all_gather | solution.py:87
  54.8 2.9 %copy-start.3 = (bf16[4,256,576]{1,2,0:T(8,128)(2,1)S(1)}, bf16[4,256,576]{1,2,0:T(8,128)(2,1)}, u32[]{:S(2)}) copy-start(bf16[4,256,576]{1,2,0:T(8,128)(2,1)} %param.11) | copy-start | bytes 3538948
  58.2 1.0 copy-start.2
  60.1 9.9 %all-to-all-start.1 = ((f32[8,1,128]{2,1,0:T(1,128)}), f32[8,1,128]{2,1,0:T(1,128)S(1)}, u32[]{:S(2)}, u32[]{:S(2)}) async-start(f32[8,1,128]{2,1,0:T(1,128)} %reshape.82), calls=%async_computation.1 | async-start | bytes 8192 | tf_op jit(solution)/shard_map/all_to_all | solution.py:110
  70.0 9.7 %all-to-all-start = ((f32[8,1,128]{2,1,0:T(1,128)}), f32[8,1,128]{2,1,0:T(1,128)S(1)}, u32[]{:S(2)}, u32[]{:S(2)}) async-start(f32[8,1,128]{2,1,0:T(1,128)} %reshape.80), calls=%async_computation | async-start | bytes 8192 | tf_op jit(solution)/shard_map/all_to_all | solution.py:109
  74.3 1.0 copy-start.1
  79.7 26.2 %all-to-all-start.2 = ((bf16[8,1,4,2,16,512]{5,4,3,2,1,0:T(8,128)(2,1)}), bf16[8,1,4,2,16,512]{5,4,3,2,1,0:T(8,128)(2,1)S(1)}, u32[]{:S(2)}, u32[]{:S(2)}) async-start(bf16[8,1,4,2,16,512]{5,4,3,2,1,0:T(8,128)(2,1)} %copy-done.1), calls=%async_computation.2 | async-start | bytes 2097152 | tf_op jit(solution)/shard_map/all_to_all | solution.py:99
  83.3 39.5 %all-gather.7.cloned.1.call-start = ((), (), s32[]{:S(2)}) async-start(), calls=%async_computation.5 | async-start | bytes 1310720 | tf_op jit(solution)/shard_map/all_gather | solution.py:10
  107.0 95.7 %reduce-scatter.4.cloned.1.call-start = ((), (), s32[]{:S(2)}) async-start(), calls=%async_computation.6 | async-start | bytes 1032192
Sparse Core Ops, SparseCore 0:
  10.2 44.5 all-gather.4
  107.1 15.5 all-gather.6
  139.0 63.6 reduce-scatter.3
